TPU v7x, 32 devices: a whole 2x2x4 slice. The times are simulated.
32 devices in a mesh: lat: 4 (over y, x), lon: 8 (over z, core).
Axes of the slice: x: 2, y: 2, z: 4, core: 2. Of those that a mesh axis runs over, the one named last changes fastest.
Arguments:
- adjoint_in: bfloat16 [8, 100, 8, 1024], P(None, None, 'lat', 'lon'), may hold values from -6 to 6
- state: bfloat16 [2, 8, 100, 8, 1024], P(None, None, None, 'lat', 'lon'), may hold values from 0.29882812 to 1
- inverses: bfloat16 [3, 8, 100, 100], replicated
- courant_lon: float32 [8, 1024], P('lat', 'lon'), may hold values from 0.1 to 0.4
- courant_lat: float32 [8, 1024], P('lat', 'lon'), may hold values from 0.1 to 0.4
- emission: float32 [100, 8, 1024], P(None, 'lat', 'lon'), may hold values from 0.02 to 0.2
- region_id: int32 [8, 1024], P('lat', 'lon'), may hold values from 0 to 31, as said below
- stiffness: int32 [8, 8, 1024], P(None, 'lat', 'lon'), may hold values from 1 to 3
Outputs:
- adjoint_out: bfloat16 [8, 100, 8, 1024], P(None, None, 'lat', 'lon')
- emission_grad: float32 [32, 100], P(('lat', 'lon'))
Inputs may be any that keep to these rules, and one draw needn't show every extreme that they name: `region_id`: constant on aligned tiles of 2 x 2 columns.
All inputs are finite; a program needn't handle non-finite values.
Results may differ from a plain program's by a relative error of at most 0.0048.
Values sent between devices are 32-bit elements; how exact they have to be, the bound alone decides.
A program may use at most 64 MiB of HBM per device.

v0:
```python
import functools

import jax
import jax.numpy as jnp
from jax import lax
from jax.experimental import pallas as pl
from jax.experimental.pallas import tpu as pltpu
from jax.sharding import PartitionSpec as P

MESH = pl.DeviceIdType.MESH
OWN1, OWN0, GHOST = 0, 1, 2


def relayed(level):
    return level // 2 % 2 == 1


def even_order(lev):
    half = lev // 2
    passed = [l for l in range(half) if relayed(l)]
    passed_merged = [l for l in range(half, lev) if relayed(l)]
    return [
        ("chem", 1, [(OWN1, l) for l in range(half, lev)]),
        ("relay", 0, passed),
        ("state", 2, half),
        ("chem", 2, [(OWN1, l) for l in range(half) if not relayed(l)]),
        ("relay", 0, passed_merged),
        ("move", 2),
        ("move", 1),
        ("chem", 3, [(OWN1, l) for l in passed]),
        ("relay", 1, passed_merged),
        ("move", 3),
        ("chem", 0, [(OWN0, l) for l in range(half) if not relayed(l)]),
        ("chem", 0, [(OWN0, l) for l in passed]),
        ("turn",),
        ("relay", 1, passed),
        ("chem", 0, [(OWN0, l) for l in range(half, lev) if not relayed(l)]),
        ("chem", 0, [(OWN0, l) for l in passed_merged]),
    ]


def odd_order(lev):
    half = lev // 2
    assert half == 4
    m = half
    batches = [
        [(GHOST, m)], [(OWN1, 0)], [(OWN1, 1)], [(OWN1, 2), (GHOST, m + 1)], [(OWN1, 3), (OWN1, m)],
        [(OWN1, m + 1), (GHOST, m + 2)], [(OWN1, m + 2), (GHOST, m + 3)], [(OWN1, m + 3)],
    ]

    def chem(n):
        return ("chem", n, batches[n - 1])

    return [
        chem(1), chem(2), ("move", 1), chem(3), ("move", 2), chem(4), ("move", 3), chem(5), ("move", 4),
        chem(6), ("move", 5), ("move", 6), chem(7), chem(8), ("move", 7), ("move", 8),
        ("chem", 0, [(OWN0, 0), (OWN0, 1)]),
        ("chem", 0, [(OWN0, m), (OWN0, m + 1)]),
        ("turn",),
        ("chem", 0, [(OWN0, m + 2), (OWN0, m + 3)]),
        ("chem", 0, [(OWN0, 2), (OWN0, 3)]),
    ]


def messages(lev):
    return 1 + max(op[1] for op in even_order(lev) + odd_order(lev) if op[0] == "chem")


def kernel(
    n_lat, n_lon,
    adj_hbm, state_hbm, inv_hbm, clon_hbm, clat_hbm, em_hbm, reg_hbm, stiff_hbm,
    outbuf, grad_ref,
    adj, state, inv, clon_ref, clat_ref, em_ref, reg_ref, stiff_ref, tall, mats,
    lamb, pbuf, vout, vin, relay, zin, st_out, st_in, cout, cin, nclon, nclat, neclat, gstiff,
    tmp, fin, coef, part, inbox1, turn, inbox2,
    adj_sem, state_sem, inv_sem, small_sem, vs, vr, rr, fs, zr, ss, sr, cs, cr, ks, kr, s1, r1, s2, r2,
):
    lev, rows2, cols = adj.shape
    nwin = state.shape[0]
    steps = inv.shape[0]
    spec = rows2 // 2
    half = lev // 2
    lat, lon = lax.axis_index("lat"), lax.axis_index("lon")
    odd = lax.rem(lat, 2) == 1
    even = lax.rem(lat, 2) == 0
    north = jnp.maximum(lat - 1, 0)
    north2 = jnp.maximum(lat - 2, 0)
    south = jnp.minimum(lat + 1, n_lat - 1)
    west = lax.rem(lon + n_lon - 1, n_lon)
    east = lax.rem(lon + 1, n_lon)
    has_north = lat > 0
    has_south = lat < n_lat - 1
    sends_ghost = lat >= 2
    passes_on = lat + 2 < n_lat
    plans = {0: even_order(lev), 1: odd_order(lev)}

    barrier = pltpu.get_barrier_semaphore()

    def greet(to):
        pl.semaphore_signal(barrier, inc=1, device_id=to, device_id_type=MESH)

    for k in range(1, n_lon):
        greet((lat, lax.rem(lon + k, n_lon)))
    for k in range(1, n_lat):
        greet((lax.rem(lat + k, n_lat), lon))

    @pl.when(has_south)
    def _():
        greet((south, west))

    @pl.when(has_north)
    def _():
        greet((north, east))

    adj_load = pltpu.make_async_copy(adj_hbm, adj, adj_sem)
    small = [
        pltpu.make_async_copy(src, dst, small_sem.at[n])
        for n, (src, dst) in enumerate((
            (clon_hbm, clon_ref), (clat_hbm, clat_ref), (stiff_hbm, stiff_ref),
            (reg_hbm, reg_ref), (em_hbm, em_ref)))
    ]
    state_loads = [
        pltpu.make_async_copy(state_hbm.at[w], state.at[w], state_sem.at[w]) for w in range(nwin)
    ]
    inv_load = pltpu.make_async_copy(inv_hbm, inv, inv_sem)
    for load in small[:2] + [adj_load, state_loads[nwin - 1], inv_load] + small[2:] + state_loads[:nwin - 1]:
        load.start()

    lane = lax.broadcasted_iota(jnp.int32, (spec, cols), 1)

    def slot_of(kind, level):
        return {OWN1: level, OWN0: lev + level, GHOST: 2 * lev + level - half}[kind]

    def after_chem(kind, level):
        return slot_of(OWN0 if kind == OWN1 else GHOST, level)

    def weights(which, names):
        return [coef[which, k, 0:1, :] for k in names]

    def remote(src, dst, send, recv, to):
        return pltpu.make_async_remote_copy(
            src_ref=src, dst_ref=dst, send_sem=send, recv_sem=recv, device_id=to, device_id_type=MESH)

    def direct(u):
        return remote(vout.at[u], vin.at[u], vs.at[u], vr.at[u], (north, lon))

    def to_relay(u):
        return remote(vout.at[u], relay.at[u], vs.at[u], rr.at[u], (north2, lon))

    def forward(u):
        return remote(relay.at[u], vin.at[u], fs.at[u], vr.at[u], (south, lon))

    def ghost_out(level):
        u, n = slot_of(GHOST, level), level - half
        return remote(vout.at[u], zin.at[n], vs.at[u], zr.at[n], (north2, lon))

    def state_out(n):
        return remote(st_out.at[n], st_in.at[n], ss.at[n], sr.at[n], (south, lon))

    def col_copy(n):
        return remote(cout.at[n], cin.at[n], cs.at[n], cr.at[n], (lat, west))

    rows_out = [
        remote(clon_ref, nclon, ks.at[0], kr.at[0], (south, lon)),
        remote(clat_ref, nclat, ks.at[1], kr.at[1], (south, lon)),
        remote(clat_ref, neclat, ks.at[2], kr.at[2], (south, west)),
    ]
    stiff_out = remote(stiff_ref, gstiff, ks.at[3], kr.at[3], (south, lon))
    mix_out = remote(coef.at[0, pl.ds(5, 4)], coef.at[1, pl.ds(5, 4)], ks.at[4], kr.at[4], (south, lon))

    def after(x):
        return pltpu.roll(x, cols - 1, 1)

    def pack(n, slots):
        message = None
        for i, (u, which) in enumerate(slots):
            c0, n0, o0, c1, o1 = weights(which, range(5))
            row0, row1 = lamb[u, 0], lamb[u, 1]
            new0 = c0 * row0 + n0 * row1 + o0 * after(row0)
            new1 = c1 * row1 + o1 * after(row1)
            for j, x in enumerate((row0, row1, new0, new1)):
                at = 4 * i + j
                message = x if at == 0 else jnp.where(lane == at, pltpu.roll(x, at, 1), message)
        cout[n] = message

    def move(u, which, n, i):
        c0, n0, o0, c1, o1, al, be, ga, de = weights(which, range(9))
        row0, row1, message = lamb[u, 0], lamb[u, 1], cin[n]

        def shift(x, j):
            edge = message if 4 * i + j == 0 else pltpu.roll(message, cols - 4 * i - j, 1)
            return after(jnp.where(lane == 0, edge, x))

        right0, right1 = shift(row0, 0), shift(row1, 1)
        new0 = c0 * row0 + n0 * row1 + o0 * right0
        new1 = c1 * row1 + o1 * right1
        pbuf[u, 0] = c0 * new0 + n0 * new1 + o0 * shift(new0, 2)
        pbuf[u, 1] = c1 * new1 + o1 * shift(new1, 3)
        v0 = al * row0
        v1 = be * row0 + ga * row1 + de * right0
        return v0, v1

    def own_sends(side, u):
        level = u % lev
        if side == 1:
            return None if u < lev and level >= half else (direct(u), None)
        return (to_relay(u) if relayed(level) else direct(u)), has_north

    def when(condition, do):
        if condition is None:
            do()
        else:
            pl.when(condition)(do)

    def transport(side, n, i, kind, level):
        u = slot_of(kind, level)
        with jax.named_scope("move"):
            v0, v1 = move(u, 1 if kind == GHOST else 0, n, i)
            if side == 1 and kind == OWN0 and level >= half:
                ghost = slot_of(GHOST, level)
                v0, v1 = v0 + pbuf[ghost, 0], v1 + pbuf[ghost, 1]
            vout[u, 0], vout[u, 1] = v0, v1
        if kind == GHOST:
            when(sends_ghost, lambda: ghost_out(level).start())
        else:
            leaving = own_sends(side, u)
            if leaving is not None:
                when(leaving[1], lambda: leaving[0].start())

    def gather(side, kind, level, i):
        u = slot_of(kind, level)
        if kind == GHOST:
            n = level - half
            with jax.named_scope("w_st"):
                state_out(n).wait_recv()
            x, y, live = [vout[level, r] for r in range(2)], [st_in[n, r] for r in range(2)], gstiff[level]
        else:
            if side == 1:
                @pl.when(has_south)
                def _():
                    with jax.named_scope("w_vin"):
                        direct(u).wait_recv()
                    extra = kind == OWN0 and level >= half
                    if extra:
                        with jax.named_scope("w_z"):
                            ghost_out(level).wait_recv()
                    for r in range(2):
                        both = vin[u, r] + zin[level - half, r] if extra else vin[u, r]
                        pbuf[u, r] = pbuf[u, r] + both
                x = [pbuf[u, r] for r in range(2)]
            elif kind == OWN0 or level < half:
                with jax.named_scope("w_vin"):
                    direct(u).wait_recv()
                x = [pbuf[u, r] + vin[u, r] for r in range(2)]
            else:
                x = [pbuf[u, r] for r in range(2)]
            tmp[i] = state[nwin - 1 if kind == OWN1 else 0, level].astype(jnp.float32)
            y, live = [tmp[i, pl.ds(r, spec, stride=2), :] for r in range(2)], stiff_ref[level]
        return (
            jnp.concatenate(x, axis=1), jnp.concatenate(y, axis=1),
            jnp.concatenate([live[0:1], live[1:2]], axis=1),
        )

    def chem(levels, gathered):
        flats, ys, lives = zip(*gathered)
        for s in reversed(range(steps)):
            mat = [mats[s, level] for level in levels]

            def dot(xs):
                return [jnp.dot(a, x.astype(jnp.bfloat16), preferred_element_type=jnp.float32) for a, x in zip(mat, xs)]

            v1 = dot(flats)
            v2 = dot([v * y for v, y in zip(v1, ys)])
            v3 = dot([v * y for v, y in zip(v2, ys)])
            flats = [
                jnp.where(live > s, 0.4 * x + 0.3 * a + 0.2 * b + 0.1 * c, x)
                for x, a, b, c, live in zip(flats, v1, v2, v3, lives)
            ]
        return flats

    def spread(k):
        to = lax.rem(lon + k, n_lon)
        return remote(part.at[to], inbox1.at[lon], s1.at[k], r1.at[lon], (lat, to))

    def spread_in(k):
        source = lax.rem(lon + k, n_lon)
        return source, remote(part.at[source], inbox1.at[source], s1.at[k], r1.at[source], (lat, source))

    def spread2(k):
        to = lax.rem(lat + k, n_lat)
        return remote(turn.at[to], inbox2.at[lat], s2.at[k], r2.at[lat], (to, lon))

    def spread2_in(k):
        source = lax.rem(lat + k, n_lat)
        return source, remote(turn.at[source], inbox2.at[source], s2.at[k], r2.at[source], (source, lon))

    def regions():
        lat8 = part.shape[1]
        contrib = jnp.concatenate([
            em_ref[pl.ds(r, spec, stride=2), :]
            * (lamb[lev, r] + fin[:, r * cols:(r + 1) * cols])
            for r in range(2)], axis=1)
        where_from = jnp.concatenate([reg_ref[0:1, :], reg_ref[1:2, :]], axis=1)
        shape = (n_lon * lat8, 2 * cols)
        column = jnp.concatenate([jnp.full((lat8, 2 * cols), c, jnp.int32) for c in range(n_lon)], axis=0)
        band = lax.broadcasted_iota(jnp.int32, (lat8, 2 * cols), 0)
        band = jnp.concatenate([band] * n_lon, axis=0)
        onehot = (jnp.broadcast_to(where_from, shape) == band * n_lon + column).astype(jnp.float32)
        sums = lax.dot_general(
            onehot, contrib, (((1,), (1,)), ((), ())),
            precision=lax.Precision.HIGHEST, preferred_element_type=jnp.float32)
        for c in range(n_lon):
            part[c] = sums[c * lat8:(c + 1) * lat8]
        for k in range(1, n_lon):
            spread(k).start()

    def regions_turn():
        total = part[lon]
        for k in range(1, n_lon):
            source, copy = spread_in(k)
            copy.wait_recv()
            total = total + inbox1[source]
        for b in range(n_lat):
            turn[b] = total[b:b + 1]
        for k in range(1, n_lat):
            spread2(k).start()

    def regions_end():
        total = turn[lat]
        for k in range(1, n_lat):
            source, copy = spread2_in(k)
            copy.wait_recv()
            total = total + inbox2[source]
        grad_ref[...] = total


    def play(side):
        sent = {}
        for op in plans[side]:
            if op[0] == "chem":
                n, items = op[1:]
                gathered = [gather(side, kind, level, i) for i, (kind, level) in enumerate(items)]
                with jax.named_scope("chem"):
                    flats = chem([level for _, level in items], gathered)
                if n:
                    slots = []
                    for (kind, level), flat in zip(items, flats):
                        u = after_chem(kind, level)
                        for r in range(2):
                            lamb[u, r] = flat[:, r * cols:(r + 1) * cols]
                        slots.append((u, 1 if kind == GHOST else 0))
                    with jax.named_scope("pack"):
                        pack(n, slots)
                    col_copy(n).start()
                    sent[n] = [(OWN0 if kind == OWN1 else GHOST, level) for kind, level in items]
                else:
                    for i, ((kind, level), flat) in enumerate(zip(items, flats)):
                        for r in range(2):
                            tmp[i, pl.ds(r, spec, stride=2), :] = flat[:, r * cols:(r + 1) * cols]
                        outbuf[level] = tmp[i].astype(jnp.bfloat16)
                        if level == 0:
                            fin[...] = flat
                            with jax.named_scope("regions"):
                                regions()
            elif op[0] == "move":
                n = op[1]
                with jax.named_scope("w_col"):
                    col_copy(n).wait_recv()
                if side == 1 and n == 1:
                    mix_out.wait_recv()
                for i, (kind, level) in enumerate(sent[n]):
                    transport(side, n, i, kind, level)
            elif op[0] == "relay":
                w, passed = op[1:]

                @pl.when(passes_on)
                def _(w=w, passed=passed):
                    for level in passed:
                        u = w * lev + level
                        with jax.named_scope("w_relay"):
                            to_relay(u).wait_recv()
                        forward(u).start()
            elif op[0] == "state":
                for k in range(op[1], op[2]):
                    state_out(k).start()
            else:
                with jax.named_scope("turn"):
                    regions_turn()

        for n in [0] + sorted(sent):
            col_copy(n).wait_send()
        for u in range(2 * lev):
            leaving = own_sends(side, u)
            if leaving is not None:
                when(leaving[1], lambda: leaving[0].wait_send())
        if side == 1:
            @pl.when(sends_ghost)
            def _():
                for level in range(half, lev):
                    ghost_out(level).wait_send()
        else:
            @pl.when(passes_on)
            def _():
                for u in range(2 * lev):
                    if relayed(u % lev):
                        forward(u).wait_send()
            stiff_out.wait_send()
            mix_out.wait_send()
            for k in range(half):
                state_out(k).wait_send()

    for load in small[:2]:
        load.wait()
    for r in range(2):
        clon, clat = clon_ref[r:r + 1, :], clat_ref[r:r + 1, :]
        coef[0, 3 * r] = jnp.broadcast_to(1.0 - clon - clat, (8, cols))
        if r == 0:
            coef[0, 1] = jnp.broadcast_to(clat, (8, cols))
        coef[0, 2 + 2 * r] = jnp.broadcast_to(clon, (8, cols))

    adj_load.wait()
    for level in range(lev):
        tmp[level % 4] = adj[level].astype(jnp.float32)
        for r in range(2):
            lamb[level, r] = tmp[level % 4, pl.ds(r, spec, stride=2), :]
    pack(0, [(level, 0) for level in range(lev)])
    state_loads[nwin - 1].wait()

    @pl.when(even)
    def _():
        for n in range(half):
            tmp[n % 4] = state[nwin - 1, half + n].astype(jnp.float32)
            for r in range(2):
                st_out[n, r] = tmp[n % 4, pl.ds(r, spec, stride=2), :]

    inv_load.wait()
    for s in range(steps):
        tall[...] = inv[s].astype(jnp.float32)
        for level in range(lev):
            mats[s, level] = tall[pl.ds(level, spec, stride=lev), :].T.astype(jnp.bfloat16)
    for load in small[2:]:
        load.wait()
    for w in range(nwin - 1):
        state_loads[w].wait()

    with jax.named_scope("w_barrier"):
        pl.semaphore_wait(
            barrier, n_lon - 1 + n_lat - 1 + has_north.astype(jnp.int32) + has_south.astype(jnp.int32))

    @pl.when(has_south)
    def _():
        for copy in rows_out:
            copy.start()
    col_copy(0).start()

    @pl.when(even)
    def _():
        stiff_out.start()
        state_out(0).start()

    @pl.when(has_north)
    def _():
        for copy in rows_out:
            copy.wait_recv()
        c0, o0, n0 = coef[0, 0], coef[0, 2], coef[0, 1]
        for r in range(2):
            clon, clat = nclon[r:r + 1, :], nclat[r:r + 1, :]
            coef[1, 3 * r] = jnp.broadcast_to(1.0 - clon - clat, (8, cols))
            if r == 0:
                coef[1, 1] = jnp.broadcast_to(clat, (8, cols))
            coef[1, 2 + 2 * r] = jnp.broadcast_to(clon, (8, cols))
        below = jnp.broadcast_to(nclat[1:2, :], (8, cols))
        beside = jnp.broadcast_to(neclat[1:2, :], (8, cols))
        first_lane = lax.broadcasted_iota(jnp.int32, (8, cols), 1) == 0
        beside = after(jnp.where(first_lane, beside, below))
        coef[0, 5] = coef[1, 1] * below
        coef[0, 6] = below * (coef[1, 3] + c0)
        coef[0, 7] = below * n0
        coef[0, 8] = below * o0 + coef[1, 4] * beside

    @pl.when(jnp.logical_not(has_north))
    def _():
        for k in range(5, 9):
            coef[0, k] = jnp.zeros((8, cols), jnp.float32)

    with jax.named_scope("w_col"):
        col_copy(0).wait_recv()

    @pl.when(even)
    def _():
        mix_out.start()
        for level in range(lev):
            transport(0, 0, level, OWN1, level)
            if level == 1:
                state_out(1).start()
        play(0)

    @pl.when(odd)
    def _():
        for level in range(lev):
            transport(1, 0, level, OWN1, level)
        stiff_out.wait_recv()
        play(1)

    @pl.when(has_south)
    def _():
        for copy in rows_out:
            copy.wait_send()
    with jax.named_scope("reg_end"):
        regions_end()
    for k in range(1, n_lon):
        spread(k).wait_send()
    for k in range(1, n_lat):
        spread2(k).wait_send()


def finish(held_ref, grad_ref, out_hbm, grad_hbm, sems):
    copies = [
        pltpu.make_async_copy(held_ref, out_hbm, sems.at[0]),
        pltpu.make_async_copy(grad_ref, grad_hbm, sems.at[1]),
    ]
    for copy in copies:
        copy.start()
    for copy in copies:
        copy.wait()


def solution(mesh):
    n_lat, n_lon = mesh.shape["lat"], mesh.shape["lon"]
    assert n_lat % 2 == 0

    def per_device(adjoint_in, state, inverses, courant_lon, courant_lat, emission, region_id, stiffness):
        lev, spec, rows, cols = adjoint_in.shape
        nwin, steps = state.shape[0], inverses.shape[0]
        assert nwin == 2 and rows == 2
        half = lev // 2
        slots = nwin * lev + half
        lat8 = -(-n_lat // 8) * 8
        f32, bf16 = jnp.float32, jnp.bfloat16
        any_space = pl.BlockSpec(memory_space=pl.ANY)
        vmem = pl.BlockSpec(memory_space=pltpu.VMEM)
        dma = pltpu.SemaphoreType.DMA

        def blocks(n):
            return pltpu.VMEM((n, rows, spec, cols), f32)

        out, grad = pl.pallas_call(
            functools.partial(kernel, n_lat, n_lon),
            out_shape=(
                pltpu.VMEM((lev, rows * spec, cols), bf16),
                pltpu.VMEM((1, spec), f32),
            ),
            in_specs=[any_space] * 8,
            out_specs=(vmem, vmem),
            scratch_shapes=[
                pltpu.VMEM((lev, rows * spec, cols), bf16),
                pltpu.VMEM((nwin, lev, rows * spec, cols), bf16),
                pltpu.VMEM((steps, spec * lev, spec), bf16),
                pltpu.VMEM(courant_lon.shape, f32),
                pltpu.VMEM(courant_lat.shape, f32),
                pltpu.VMEM((spec * rows, cols), f32),
                pltpu.VMEM(region_id.shape, jnp.int32),
                pltpu.VMEM(stiffness.shape, jnp.int32),
                pltpu.VMEM((spec * lev, spec), f32),
                pltpu.VMEM(inverses.shape, bf16),
                blocks(slots), blocks(slots), blocks(slots),
                blocks(nwin * lev), blocks(nwin * lev), blocks(half), blocks(half), blocks(half),
                pltpu.VMEM((messages(lev), spec, cols), f32),
                pltpu.VMEM((messages(lev), spec, cols), f32),
                pltpu.VMEM(courant_lon.shape, f32),
                pltpu.VMEM(courant_lat.shape, f32),
                pltpu.VMEM(courant_lat.shape, f32),
                pltpu.VMEM(stiffness.shape, jnp.int32),
                pltpu.VMEM((4, rows * spec, cols), f32),
                pltpu.VMEM((spec, rows * cols), f32),
                pltpu.VMEM((2, 9, 8, cols), f32),
                pltpu.VMEM((n_lon, lat8, spec), f32),
                pltpu.VMEM((n_lon, lat8, spec), f32),
                pltpu.VMEM((n_lat, 1, spec), f32),
                pltpu.VMEM((n_lat, 1, spec), f32),
                dma, dma((nwin,)), dma, dma((5,)),
                dma((slots,)), dma((nwin * lev,)), dma((nwin * lev,)), dma((nwin * lev,)), dma((half,)),
                dma((half,)), dma((half,)),
                dma((messages(lev),)), dma((messages(lev),)), dma((5,)), dma((5,)),
                dma((n_lon,)), dma((n_lon,)), dma((n_lat,)), dma((n_lat,)),
            ],
            compiler_params=pltpu.CompilerParams(collective_id=0, has_side_effects=True),
        )(
            adjoint_in.reshape(lev, spec * rows, cols),
            state.reshape(nwin, lev, spec * rows, cols),
            inverses.transpose(0, 2, 1, 3).reshape(steps, spec * lev, spec), courant_lon, courant_lat,
            emission.reshape(spec * rows, cols), region_id, stiffness,
        )
        out, grad = pl.pallas_call(
            finish,
            out_shape=(
                jax.ShapeDtypeStruct(out.shape, bf16),
                jax.ShapeDtypeStruct(grad.shape, f32),
            ),
            in_specs=[any_space] * 2,
            out_specs=(any_space, any_space),
            scratch_shapes=[dma((2,))],
        )(*(pltpu.with_memory_space_constraint(x, pltpu.VMEM) for x in (out, grad)))
        return out.reshape(adjoint_in.shape), grad

    in_specs = (
        P(None, None, "lat", "lon"),
        P(None, None, None, "lat", "lon"),
        P(),
        P("lat", "lon"),
        P("lat", "lon"),
        P(None, "lat", "lon"),
        P("lat", "lon"),
        P(None, "lat", "lon"),
    )
    out_specs = (P(None, None, "lat", "lon"), P(("lat", "lon"), None))
    return jax.shard_map(
        per_device, mesh=mesh, in_specs=in_specs, out_specs=out_specs, check_vma=False
    )
```

profile of v0, /device:TPU:0, one launch (start us, length us, event | category | flops | bytes accessed | tf_op | source)
XLA Modules:
  0.0 46.3 jit_solution(6512565011202562468)
XLA Ops:
  0.6 44.7 %shard_map.95 = (bf16[8,200,128]{2,1,0:T(8,128)(2,1)S(1)}, f32[1,100]{1,0:T(1,128)S(1)}) custom-call(bf16[8,200,128]{2,1,0:T(8,128)(2,1)} %bitcast.9, bf16[2,8,200,128]{3,2,1,0:T(8,128)(2,1)} %bitcast.7, bf16[3,800,100]{2,1,0:T(8,128)(2,1)} %bitcast.8, f32[2,128]{1,0:T(2,128)} %clon_hbm.1, f32[2,128]{1,0:T(2,128)} %clat_hbm.1, f32[200,128]{1,0:T(8,128)} %bitcast.10, ...), custom_call_target="tpu_custom_call" | custom-call | tf_op jit(solution)/shard_map/pallas_call | solution.py:547
  45.4 0.8 %shard_map.96 = (bf16[8,200,128]{2,1,0:T(8,128)(2,1)}, f32[1,100]{1,0:T(1,128)}) custom-call(bf16[8,200,128]{2,1,0:T(8,128)(2,1)S(1)} %get-tuple-element.6.held_ref, f32[1,100]{1,0:T(1,128)S(1)} %get-tuple-element.7.grad_ref), custom_call_target="tpu_custom_call" | custom-call | tf_op jit(solution)/shard_map/pallas_call | solution.py:594
where the time goes:
time: 46.5 us; the launch traced here: 46.3 us
  Pallas kernels  45.5 us (98%)
  between operations  0.82 us (2%)
    pallas_call x1, Pallas kernels, per_device(): pl.pallas_call(functools.partial(kernel, n_lat, n_lon), out_shape=(pltpu....  44.7 us

commit v1 on v0

--- a/solution.py
+++ b/solution.py
@@ -11,8 +11,8 @@
 OWN1, OWN0, GHOST = 0, 1, 2
 
 
-def relayed(level):
-    return level // 2 % 2 == 1
+def relayed(level, window=0):
+    return level // 2 % 2 == 1 or (window == 1 and level == 1)
 
 
 def even_order(lev):
@@ -20,17 +20,22 @@
     passed = [l for l in range(half) if relayed(l)]
     passed_merged = [l for l in range(half, lev) if relayed(l)]
     return [
+        ("first", list(range(half, lev))),
+        ("relay", 0, passed[:1]),
         ("chem", 1, [(OWN1, l) for l in range(half, lev)]),
-        ("relay", 0, passed),
-        ("state", 2, half),
+        ("relay", 0, passed[1:]),
+        ("state", 2, half - 1),
+        ("first", list(range(half))),
         ("chem", 2, [(OWN1, l) for l in range(half) if not relayed(l)]),
         ("relay", 0, passed_merged),
+        ("state", half - 1, half),
+        ("chem", 3, [(OWN1, l) for l in passed]),
         ("move", 2),
         ("move", 1),
-        ("chem", 3, [(OWN1, l) for l in passed]),
-        ("relay", 1, passed_merged),
         ("move", 3),
         ("chem", 0, [(OWN0, l) for l in range(half) if not relayed(l)]),
+        ("relay", 1, [l for l in range(half) if relayed(l, 1) and not relayed(l)]),
+        ("relay", 1, passed_merged),
         ("chem", 0, [(OWN0, l) for l in passed]),
         ("turn",),
         ("relay", 1, passed),
@@ -44,21 +49,23 @@
     assert half == 4
     m = half
     batches = [
-        [(GHOST, m)], [(OWN1, 0)], [(OWN1, 1)], [(OWN1, 2), (GHOST, m + 1)], [(OWN1, 3), (OWN1, m)],
-        [(OWN1, m + 1), (GHOST, m + 2)], [(OWN1, m + 2), (GHOST, m + 3)], [(OWN1, m + 3)],
+        [(OWN1, 0)], [(OWN1, 1)], [(GHOST, m), (OWN1, 2)], [(OWN1, 3), (OWN1, m)],
+        [(GHOST, m + 1), (OWN1, m + 1)], [(GHOST, m + 2), (OWN1, m + 2)], [(GHOST, m + 3), (OWN1, m + 3)],
     ]
 
     def chem(n):
         return ("chem", n, batches[n - 1])
 
     return [
-        chem(1), chem(2), ("move", 1), chem(3), ("move", 2), chem(4), ("move", 3), chem(5), ("move", 4),
-        chem(6), ("move", 5), ("move", 6), chem(7), chem(8), ("move", 7), ("move", 8),
-        ("chem", 0, [(OWN0, 0), (OWN0, 1)]),
-        ("chem", 0, [(OWN0, m), (OWN0, m + 1)]),
+        ("first", [0]), chem(1), ("first", [1]), chem(2), ("first", list(range(2, lev))),
+        ("move", 1), chem(3), ("move", 2), chem(4), ("move", 3), chem(5), ("move", 4),
+        chem(6), ("move", 5), chem(7), ("move", 6),
+        ("chem", 0, [(OWN0, 0)]),
+        ("move", 7),
+        ("chem", 0, [(OWN0, 1), (OWN0, m)]),
         ("turn",),
-        ("chem", 0, [(OWN0, m + 2), (OWN0, m + 3)]),
-        ("chem", 0, [(OWN0, 2), (OWN0, 3)]),
+        ("chem", 0, [(OWN0, m + 1), (OWN0, m + 2)]),
+        ("chem", 0, [(OWN0, 2), (OWN0, 3), (OWN0, m + 3)]),
     ]
 
 
@@ -71,9 +78,9 @@
     adj_hbm, state_hbm, inv_hbm, clon_hbm, clat_hbm, em_hbm, reg_hbm, stiff_hbm,
     outbuf, grad_ref,
     adj, state, inv, clon_ref, clat_ref, em_ref, reg_ref, stiff_ref, tall, mats,
-    lamb, pbuf, vout, vin, relay, zin, st_out, st_in, cout, cin, nclon, nclat, neclat, gstiff,
-    tmp, fin, coef, part, inbox1, turn, inbox2,
-    adj_sem, state_sem, inv_sem, small_sem, vs, vr, rr, fs, zr, ss, sr, cs, cr, ks, kr, s1, r1, s2, r2,
+    lamb, pbuf, vout, vin, relay, zin, st_out, st_in, cout, cin, nclon, nclat, neclat, sclon, sclat, eclat, gstiff, corner_end, corner_in, corner,
+    tmp, fin, coef, mixed, part, inbox1, turn, inbox2,
+    adj_sem, state_sem, inv_sem, small_sem, vs, vr, rr, fs, zr, ss, sr, cs, cr, ks, kr, ds, dr, s1, r1, s2, r2,
 ):
     lev, rows2, cols = adj.shape
     nwin = state.shape[0]
@@ -107,10 +114,12 @@
     @pl.when(has_south)
     def _():
         greet((south, west))
+        greet((south, east))
 
     @pl.when(has_north)
     def _():
         greet((north, east))
+        greet((north, west))
 
     adj_load = pltpu.make_async_copy(adj_hbm, adj, adj_sem)
     small = [
@@ -141,11 +150,14 @@
         return pltpu.make_async_remote_copy(
             src_ref=src, dst_ref=dst, send_sem=send, recv_sem=recv, device_id=to, device_id_type=MESH)
 
+    def leaves(u):
+        return (lamb if u < lev else vout).at[u]
+
     def direct(u):
-        return remote(vout.at[u], vin.at[u], vs.at[u], vr.at[u], (north, lon))
+        return remote(leaves(u), vin.at[u], vs.at[u], vr.at[u], (north, lon))
 
     def to_relay(u):
-        return remote(vout.at[u], relay.at[u], vs.at[u], rr.at[u], (north2, lon))
+        return remote(leaves(u), relay.at[u], vs.at[u], rr.at[u], (north2, lon))
 
     def forward(u):
         return remote(relay.at[u], vin.at[u], fs.at[u], vr.at[u], (south, lon))
@@ -165,6 +177,12 @@
         remote(clat_ref, nclat, ks.at[1], kr.at[1], (south, lon)),
         remote(clat_ref, neclat, ks.at[2], kr.at[2], (south, west)),
     ]
+    rows_north = [
+        remote(clon_ref, sclon, ks.at[5], kr.at[5], (north, lon)),
+        remote(clat_ref, sclat, ks.at[6], kr.at[6], (north, lon)),
+    ]
+    rows_west = remote(clat_ref, eclat, ks.at[7], kr.at[7], (lat, west))
+    corner_out = remote(corner_end, corner_in, ds, dr, (north, west))
     stiff_out = remote(stiff_ref, gstiff, ks.at[3], kr.at[3], (south, lon))
     mix_out = remote(coef.at[0, pl.ds(5, 4)], coef.at[1, pl.ds(5, 4)], ks.at[4], kr.at[4], (south, lon))
 
@@ -183,7 +201,7 @@
                 message = x if at == 0 else jnp.where(lane == at, pltpu.roll(x, at, 1), message)
         cout[n] = message
 
-    def move(u, which, n, i):
+    def move(u, which, n, i, combine):
         c0, n0, o0, c1, o1, al, be, ga, de = weights(which, range(9))
         row0, row1, message = lamb[u, 0], lamb[u, 1], cin[n]
 
@@ -196,6 +214,8 @@
         new1 = c1 * row1 + o1 * right1
         pbuf[u, 0] = c0 * new0 + n0 * new1 + o0 * shift(new0, 2)
         pbuf[u, 1] = c1 * new1 + o1 * shift(new1, 3)
+        if not combine:
+            return None
         v0 = al * row0
         v1 = be * row0 + ga * row1 + de * right0
         return v0, v1
@@ -204,7 +224,7 @@
         level = u % lev
         if side == 1:
             return None if u < lev and level >= half else (direct(u), None)
-        return (to_relay(u) if relayed(level) else direct(u)), has_north
+        return (to_relay(u) if relayed(level, u // lev) else direct(u)), has_north
 
     def when(condition, do):
         if condition is None:
@@ -214,18 +234,30 @@
 
     def transport(side, n, i, kind, level):
         u = slot_of(kind, level)
+        combine = kind != OWN1 or (side == 1 and level >= half)
         with jax.named_scope("move"):
-            v0, v1 = move(u, 1 if kind == GHOST else 0, n, i)
-            if side == 1 and kind == OWN0 and level >= half:
-                ghost = slot_of(GHOST, level)
-                v0, v1 = v0 + pbuf[ghost, 0], v1 + pbuf[ghost, 1]
-            vout[u, 0], vout[u, 1] = v0, v1
+            both = move(u, 1 if kind == GHOST else 0, n, i, combine)
+            if combine:
+                if side == 1 and kind == OWN0 and level >= half:
+                    ghost = slot_of(GHOST, level)
+                    both = both[0] + pbuf[ghost, 0], both[1] + pbuf[ghost, 1]
+                vout[u, 0], vout[u, 1] = both
         if kind == GHOST:
             when(sends_ghost, lambda: ghost_out(level).start())
-        else:
-            leaving = own_sends(side, u)
-            if leaving is not None:
-                when(leaving[1], lambda: leaving[0].start())
+        elif kind == OWN0:
+            send(side, u)
+
+    def send(side, u):
+        leaving = own_sends(side, u)
+        if leaving is not None:
+            when(leaving[1], lambda: leaving[0].start())
+
+    def arrived(level):
+        al, be, ga, de = [mixed[k, 0:1, :] for k in range(4)]
+        row0, row1, message = vin[level, 0], vin[level, 1], corner[...]
+        edge = message if level == 0 else pltpu.roll(message, cols - 4 * level, 1)
+        right0 = after(jnp.where(lane == 0, edge, row0))
+        return al * row0, be * row0 + ga * row1 + de * right0
 
     def gather(side, kind, level, i):
         u = slot_of(kind, level)
@@ -233,6 +265,8 @@
             n = level - half
             with jax.named_scope("w_st"):
                 state_out(n).wait_recv()
+            if n == 0:
+                stiff_out.wait_recv()
             x, y, live = [vout[level, r] for r in range(2)], [st_in[n, r] for r in range(2)], gstiff[level]
         else:
             if side == 1:
@@ -244,14 +278,16 @@
                     if extra:
                         with jax.named_scope("w_z"):
                             ghost_out(level).wait_recv()
+                    adds = arrived(level) if kind == OWN1 else [vin[u, r] for r in range(2)]
                     for r in range(2):
-                        both = vin[u, r] + zin[level - half, r] if extra else vin[u, r]
+                        both = adds[r] + zin[level - half, r] if extra else adds[r]
                         pbuf[u, r] = pbuf[u, r] + both
                 x = [pbuf[u, r] for r in range(2)]
             elif kind == OWN0 or level < half:
                 with jax.named_scope("w_vin"):
                     direct(u).wait_recv()
-                x = [pbuf[u, r] + vin[u, r] for r in range(2)]
+                adds = arrived(level) if kind == OWN1 else [vin[u, r] for r in range(2)]
+                x = [pbuf[u, r] + adds[r] for r in range(2)]
             else:
                 x = [pbuf[u, r] for r in range(2)]
             tmp[i] = state[nwin - 1 if kind == OWN1 else 0, level].astype(jnp.float32)
@@ -362,11 +398,14 @@
                             fin[...] = flat
                             with jax.named_scope("regions"):
                                 regions()
+            elif op[0] == "first":
+                for level in op[1]:
+                    transport(side, 0, level, OWN1, level)
             elif op[0] == "move":
                 n = op[1]
                 with jax.named_scope("w_col"):
                     col_copy(n).wait_recv()
-                if side == 1 and n == 1:
+                if side == 1 and n == 3:
                     mix_out.wait_recv()
                 for i, (kind, level) in enumerate(sent[n]):
                     transport(side, n, i, kind, level)
@@ -382,7 +421,7 @@
                         forward(u).start()
             elif op[0] == "state":
                 for k in range(op[1], op[2]):
-                    state_out(k).start()
+                    give_state(k)
             else:
                 with jax.named_scope("turn"):
                     regions_turn()
@@ -402,7 +441,7 @@
             @pl.when(passes_on)
             def _():
                 for u in range(2 * lev):
-                    if relayed(u % lev):
+                    if relayed(u % lev, u // lev):
                         forward(u).wait_send()
             stiff_out.wait_send()
             mix_out.wait_send()
@@ -423,40 +462,78 @@
         tmp[level % 4] = adj[level].astype(jnp.float32)
         for r in range(2):
             lamb[level, r] = tmp[level % 4, pl.ds(r, spec, stride=2), :]
-    pack(0, [(level, 0) for level in range(lev)])
+    with jax.named_scope("pack"):
+        pack(0, [(level, 0) for level in range(lev)])
+        corner_end[...] = jnp.concatenate(
+            [cout[0], jnp.zeros((cols - spec, cols), jnp.float32)], axis=0).T[:4 * lev]
+    with jax.named_scope("w_barrier"):
+        pl.semaphore_wait(
+            barrier, n_lon - 1 + n_lat - 1 + 2 * has_north.astype(jnp.int32) + 2 * has_south.astype(jnp.int32))
+
+    @pl.when(has_south)
+    def _():
+        for copy in rows_out:
+            copy.start()
+
+    @pl.when(has_north)
+    def _():
+        for copy in rows_north:
+            copy.start()
+    rows_west.start()
+
+    @pl.when(even)
+    def _():
+        send(0, 0)
+        send(0, 2)
+
+    @pl.when(odd)
+    def _():
+        send(1, 0)
+    col_copy(0).start()
+
+    @pl.when(has_north)
+    def _():
+        corner_out.start()
+
+    def give_state(n):
+        tmp[n % 4] = state[nwin - 1, half + n].astype(jnp.float32)
+        for r in range(2):
+            st_out[n, r] = tmp[n % 4, pl.ds(r, spec, stride=2), :]
+        state_out(n).start()
+
     state_loads[nwin - 1].wait()
 
     @pl.when(even)
     def _():
-        for n in range(half):
-            tmp[n % 4] = state[nwin - 1, half + n].astype(jnp.float32)
-            for r in range(2):
-                st_out[n, r] = tmp[n % 4, pl.ds(r, spec, stride=2), :]
+        for level in range(1, half):
+            if level != 2:
+                send(0, level)
+        give_state(0)
+        send(0, half)
+        for level in range(half, lev):
+            if relayed(level):
+                send(0, level)
+
+    @pl.when(odd)
+    def _():
+        for level in range(1, half):
+            send(1, level)
 
     inv_load.wait()
-    for s in range(steps):
-        tall[...] = inv[s].astype(jnp.float32)
-        for level in range(lev):
-            mats[s, level] = tall[pl.ds(level, spec, stride=lev), :].T.astype(jnp.bfloat16)
+    with jax.named_scope("mats"):
+        for s in range(steps):
+            tall[...] = inv[s].astype(jnp.float32)
+            for level in range(lev):
+                mats[s, level] = tall[pl.ds(level, spec, stride=lev), :].T.astype(jnp.bfloat16)
     for load in small[2:]:
         load.wait()
     for w in range(nwin - 1):
         state_loads[w].wait()
-
-    with jax.named_scope("w_barrier"):
-        pl.semaphore_wait(
-            barrier, n_lon - 1 + n_lat - 1 + has_north.astype(jnp.int32) + has_south.astype(jnp.int32))
-
-    @pl.when(has_south)
-    def _():
-        for copy in rows_out:
-            copy.start()
-    col_copy(0).start()
-
-    @pl.when(even)
-    def _():
-        stiff_out.start()
-        state_out(0).start()
+    first_lane = lax.broadcasted_iota(jnp.int32, (8, cols), 1) == 0
+
+    def beside(row, next_row):
+        row, next_row = jnp.broadcast_to(row, (8, cols)), jnp.broadcast_to(next_row, (8, cols))
+        return after(jnp.where(first_lane, next_row, row))
 
     @pl.when(has_north)
     def _():
@@ -470,37 +547,63 @@
                 coef[1, 1] = jnp.broadcast_to(clat, (8, cols))
             coef[1, 2 + 2 * r] = jnp.broadcast_to(clon, (8, cols))
         below = jnp.broadcast_to(nclat[1:2, :], (8, cols))
-        beside = jnp.broadcast_to(neclat[1:2, :], (8, cols))
-        first_lane = lax.broadcasted_iota(jnp.int32, (8, cols), 1) == 0
-        beside = after(jnp.where(first_lane, beside, below))
         coef[0, 5] = coef[1, 1] * below
         coef[0, 6] = below * (coef[1, 3] + c0)
         coef[0, 7] = below * n0
-        coef[0, 8] = below * o0 + coef[1, 4] * beside
+        coef[0, 8] = below * o0 + coef[1, 4] * beside(nclat[1:2, :], neclat[1:2, :])
 
     @pl.when(jnp.logical_not(has_north))
     def _():
         for k in range(5, 9):
             coef[0, k] = jnp.zeros((8, cols), jnp.float32)
 
+    rows_west.wait_recv()
+
+    @pl.when(has_south)
+    def _():
+        for copy in rows_north:
+            copy.wait_recv()
+        clon, clat = sclon[0:1, :], sclat[0:1, :]
+        below = jnp.broadcast_to(clat_ref[1:2, :], (8, cols))
+        mixed[0] = coef[0, 1] * below
+        mixed[1] = below * (coef[0, 3] + jnp.broadcast_to(1.0 - clon - clat, (8, cols)))
+        mixed[2] = below * jnp.broadcast_to(clat, (8, cols))
+        mixed[3] = below * jnp.broadcast_to(clon, (8, cols)) + coef[0, 4] * beside(clat_ref[1:2, :], eclat[1:2, :])
+
+    @pl.when(even)
+    def _():
+        mix_out.start()
+        stiff_out.start()
+        give_state(1)
+        for level in range(half + 1, lev):
+            if not relayed(level):
+                send(0, level)
+
+    @pl.when(has_south)
+    def _():
+        with jax.named_scope("w_corner"):
+            corner_out.wait_recv()
+        corner[...] = jnp.concatenate(
+            [corner_in[...], jnp.zeros((cols - 4 * lev, cols), jnp.float32)], axis=0).T[:spec]
+
     with jax.named_scope("w_col"):
         col_copy(0).wait_recv()
 
     @pl.when(even)
     def _():
-        mix_out.start()
-        for level in range(lev):
-            transport(0, 0, level, OWN1, level)
-            if level == 1:
-                state_out(1).start()
         play(0)
 
     @pl.when(odd)
     def _():
-        for level in range(lev):
-            transport(1, 0, level, OWN1, level)
-        stiff_out.wait_recv()
         play(1)
+
+    rows_west.wait_send()
+
+    @pl.when(has_north)
+    def _():
+        corner_out.wait_send()
+        for copy in rows_north:
+            copy.wait_send()
 
     @pl.when(has_south)
     def _():
@@ -570,10 +673,17 @@
                 pltpu.VMEM(courant_lon.shape, f32),
                 pltpu.VMEM(courant_lat.shape, f32),
                 pltpu.VMEM(courant_lat.shape, f32),
+                pltpu.VMEM(courant_lon.shape, f32),
+                pltpu.VMEM(courant_lat.shape, f32),
+                pltpu.VMEM(courant_lat.shape, f32),
                 pltpu.VMEM(stiffness.shape, jnp.int32),
+                pltpu.VMEM((4 * lev, cols), f32),
+                pltpu.VMEM((4 * lev, cols), f32),
+                pltpu.VMEM((spec, cols), f32),
                 pltpu.VMEM((4, rows * spec, cols), f32),
                 pltpu.VMEM((spec, rows * cols), f32),
                 pltpu.VMEM((2, 9, 8, cols), f32),
+                pltpu.VMEM((4, 8, cols), f32),
                 pltpu.VMEM((n_lon, lat8, spec), f32),
                 pltpu.VMEM((n_lon, lat8, spec), f32),
                 pltpu.VMEM((n_lat, 1, spec), f32),
@@ -581,7 +691,7 @@
                 dma, dma((nwin,)), dma, dma((5,)),
                 dma((slots,)), dma((nwin * lev,)), dma((nwin * lev,)), dma((nwin * lev,)), dma((half,)),
                 dma((half,)), dma((half,)),
-                dma((messages(lev),)), dma((messages(lev),)), dma((5,)), dma((5,)),
+                dma((messages(lev),)), dma((messages(lev),)), dma((8,)), dma((8,)), dma, dma,
                 dma((n_lon,)), dma((n_lon,)), dma((n_lat,)), dma((n_lat,)),
             ],
             compiler_params=pltpu.CompilerParams(collective_id=0, has_side_effects=True),

time: 46.5 us -> 42.9 us (0.923)
  the two profiles are of different devices: /device:TPU:0 before, /device:TPU:3 now
where the time goes in v1:
time: 42.9 us; the launch traced here: 42.7 us
  Pallas kernels  41.9 us (98%)
  between operations  0.82 us (2%)
    pallas_call x1, Pallas kernels, per_device(): pl.pallas_call(functools.partial(kernel, n_lat, n_lon), out_shape=(pltpu....  41.1 us

profile of v1, /device:TPU:3, one launch (start us, length us, event | category | flops | bytes accessed | tf_op | source)
XLA Modules:
  0.0 42.7 jit_solution(1938828104580170445)
XLA Ops:
  0.6 41.1 %shard_map.95 = (bf16[8,200,128]{2,1,0:T(8,128)(2,1)S(1)}, f32[1,100]{1,0:T(1,128)S(1)}) custom-call(bf16[8,200,128]{2,1,0:T(8,128)(2,1)} %bitcast.9, bf16[2,8,200,128]{3,2,1,0:T(8,128)(2,1)} %bitcast.7, bf16[3,800,100]{2,1,0:T(8,128)(2,1)} %bitcast.8, f32[2,128]{1,0:T(2,128)} %clon_hbm.1, f32[2,128]{1,0:T(2,128)} %clat_hbm.1, f32[200,128]{1,0:T(8,128)} %bitcast.10, ...), custom_call_target="tpu_custom_call" | custom-call | tf_op jit(solution)/shard_map/pallas_call | solution.py:650
  41.8 0.8 %shard_map.96 = (bf16[8,200,128]{2,1,0:T(8,128)(2,1)}, f32[1,100]{1,0:T(1,128)}) custom-call(bf16[8,200,128]{2,1,0:T(8,128)(2,1)S(1)} %get-tuple-element.6.held_ref, f32[1,100]{1,0:T(1,128)S(1)} %get-tuple-element.7.grad_ref), custom_call_target="tpu_custom_call" | custom-call | tf_op jit(solution)/shard_map/pallas_call | solution.py:704

commit v2 on v1

--- a/solution.py
+++ b/solution.py
@@ -29,9 +29,10 @@
         ("chem", 2, [(OWN1, l) for l in range(half) if not relayed(l)]),
         ("relay", 0, passed_merged),
         ("state", half - 1, half),
+        ("move", 1),
         ("chem", 3, [(OWN1, l) for l in passed]),
         ("move", 2),
-        ("move", 1),
+        ("send", [l for l in range(half, lev) if not relayed(l)]),
         ("move", 3),
         ("chem", 0, [(OWN0, l) for l in range(half) if not relayed(l)]),
         ("relay", 1, [l for l in range(half) if relayed(l, 1) and not relayed(l)]),
@@ -40,6 +41,7 @@
         ("turn",),
         ("relay", 1, passed),
         ("chem", 0, [(OWN0, l) for l in range(half, lev) if not relayed(l)]),
+        ("drain",),
         ("chem", 0, [(OWN0, l) for l in passed_merged]),
     ]
 
@@ -57,14 +59,15 @@
         return ("chem", n, batches[n - 1])
 
     return [
-        ("first", [0]), chem(1), ("first", [1]), chem(2), ("first", list(range(2, lev))),
-        ("move", 1), chem(3), ("move", 2), chem(4), ("move", 3), chem(5), ("move", 4),
-        chem(6), ("move", 5), chem(7), ("move", 6),
+        ("first", [0]), chem(1), ("first", [1]), chem(2), ("first", [2, m]), chem(3), ("move", 1),
+        ("first", [3]), chem(4), ("move", 2), ("first", [m + 1, m + 2, m + 3]), ("move", 3),
+        chem(5), ("move", 4),        chem(6), chem(7), ("move", 5),
         ("chem", 0, [(OWN0, 0)]),
-        ("move", 7),
+        ("move", 6), ("move", 7),
         ("chem", 0, [(OWN0, 1), (OWN0, m)]),
         ("turn",),
         ("chem", 0, [(OWN0, m + 1), (OWN0, m + 2)]),
+        ("drain",),
         ("chem", 0, [(OWN0, 2), (OWN0, 3), (OWN0, m + 3)]),
     ]
 
@@ -99,6 +102,7 @@
     has_south = lat < n_lat - 1
     sends_ghost = lat >= 2
     passes_on = lat + 2 < n_lat
+    passing = [u for u in range(2 * lev) if relayed(u % lev, u // lev)]
     plans = {0: even_order(lev), 1: odd_order(lev)}
 
     barrier = pltpu.get_barrier_semaphore()
@@ -154,23 +158,24 @@
         return (lamb if u < lev else vout).at[u]
 
     def direct(u):
-        return remote(leaves(u), vin.at[u], vs.at[u], vr.at[u], (north, lon))
+        return remote(leaves(u), vin.at[u], vs, vr.at[u], (north, lon))
 
     def to_relay(u):
-        return remote(leaves(u), relay.at[u], vs.at[u], rr.at[u], (north2, lon))
+        n = passing.index(u)
+        return remote(leaves(u), relay.at[n], vs, rr.at[n], (north2, lon))
 
     def forward(u):
-        return remote(relay.at[u], vin.at[u], fs.at[u], vr.at[u], (south, lon))
+        return remote(relay.at[passing.index(u)], vin.at[u], fs, vr.at[u], (south, lon))
 
     def ghost_out(level):
         u, n = slot_of(GHOST, level), level - half
-        return remote(vout.at[u], zin.at[n], vs.at[u], zr.at[n], (north2, lon))
+        return remote(vout.at[u], zin.at[n], vs, zr.at[n], (north2, lon))
 
     def state_out(n):
-        return remote(st_out.at[n], st_in.at[n], ss.at[n], sr.at[n], (south, lon))
+        return remote(st_out.at[n], st_in.at[n], ss, sr.at[n], (south, lon))
 
     def col_copy(n):
-        return remote(cout.at[n], cin.at[n], cs.at[n], cr.at[n], (lat, west))
+        return remote(cout.at[n], cin.at[n], cs, cr.at[n], (lat, west))
 
     rows_out = [
         remote(clon_ref, nclon, ks.at[0], kr.at[0], (south, lon)),
@@ -244,7 +249,7 @@
                 vout[u, 0], vout[u, 1] = both
         if kind == GHOST:
             when(sends_ghost, lambda: ghost_out(level).start())
-        elif kind == OWN0:
+        elif kind == OWN0 and not (side == 0 and level >= half and not relayed(level)):
             send(side, u)
 
     def send(side, u):
@@ -316,19 +321,19 @@
 
     def spread(k):
         to = lax.rem(lon + k, n_lon)
-        return remote(part.at[to], inbox1.at[lon], s1.at[k], r1.at[lon], (lat, to))
-
-    def spread_in(k):
-        source = lax.rem(lon + k, n_lon)
-        return source, remote(part.at[source], inbox1.at[source], s1.at[k], r1.at[source], (lat, source))
+        return remote(part.at[to], inbox1.at[k - 1], s1, r1, (lat, to))
+
+    def spread_all():
+        n = pl.ds(0, n_lon - 1)
+        return remote(part.at[n], inbox1.at[n], s1, r1, (lat, west))
 
     def spread2(k):
         to = lax.rem(lat + k, n_lat)
-        return remote(turn.at[to], inbox2.at[lat], s2.at[k], r2.at[lat], (to, lon))
-
-    def spread2_in(k):
-        source = lax.rem(lat + k, n_lat)
-        return source, remote(turn.at[source], inbox2.at[source], s2.at[k], r2.at[source], (source, lon))
+        return remote(turn.at[to], inbox2.at[k - 1], s2, r2, (to, lon))
+
+    def spread2_all():
+        n = pl.ds(0, n_lat - 1)
+        return remote(turn.at[n], inbox2.at[n], s2, r2, (north, lon))
 
     def regions():
         lat8 = part.shape[1]
@@ -352,10 +357,9 @@
 
     def regions_turn():
         total = part[lon]
-        for k in range(1, n_lon):
-            source, copy = spread_in(k)
-            copy.wait_recv()
-            total = total + inbox1[source]
+        spread_all().wait_recv()
+        for k in range(n_lon - 1):
+            total = total + inbox1[k]
         for b in range(n_lat):
             turn[b] = total[b:b + 1]
         for k in range(1, n_lat):
@@ -363,12 +367,43 @@
 
     def regions_end():
         total = turn[lat]
-        for k in range(1, n_lat):
-            source, copy = spread2_in(k)
-            copy.wait_recv()
-            total = total + inbox2[source]
+        spread2_all().wait_recv()
+        for k in range(n_lat - 1):
+            total = total + inbox2[k]
         grad_ref[...] = total
 
+    def drain(side, sent):
+        n = 1 + len(sent)
+        remote(cout.at[pl.ds(0, n)], cin.at[pl.ds(0, n)], cs, cr.at[0], (lat, west)).wait_send()
+
+        def left(n):
+            remote(lamb.at[pl.ds(0, n)], vin.at[pl.ds(0, n)], vs, vr.at[0], (north, lon)).wait_send()
+
+        if side == 1:
+            left(lev + half)
+
+            @pl.when(sends_ghost)
+            def _():
+                left(half)
+        else:
+            @pl.when(has_north)
+            def _():
+                left(2 * lev)
+            stiff_out.wait_send()
+            mix_out.wait_send()
+            remote(st_out, st_in, ss, sr.at[0], (south, lon)).wait_send()
+        rows_west.wait_send()
+
+        @pl.when(has_north)
+        def _():
+            corner_out.wait_send()
+            for copy in rows_north:
+                copy.wait_send()
+
+        @pl.when(has_south)
+        def _():
+            for copy in rows_out:
+                copy.wait_send()
 
     def play(side):
         sent = {}
@@ -398,6 +433,9 @@
                             fin[...] = flat
                             with jax.named_scope("regions"):
                                 regions()
+            elif op[0] == "send":
+                for level in op[1]:
+                    send(side, lev + level)
             elif op[0] == "first":
                 for level in op[1]:
                     transport(side, 0, level, OWN1, level)
@@ -422,31 +460,16 @@
             elif op[0] == "state":
                 for k in range(op[1], op[2]):
                     give_state(k)
+            elif op[0] == "drain":
+                drain(side, sent)
             else:
                 with jax.named_scope("turn"):
                     regions_turn()
 
-        for n in [0] + sorted(sent):
-            col_copy(n).wait_send()
-        for u in range(2 * lev):
-            leaving = own_sends(side, u)
-            if leaving is not None:
-                when(leaving[1], lambda: leaving[0].wait_send())
-        if side == 1:
-            @pl.when(sends_ghost)
-            def _():
-                for level in range(half, lev):
-                    ghost_out(level).wait_send()
-        else:
+        if side == 0:
             @pl.when(passes_on)
             def _():
-                for u in range(2 * lev):
-                    if relayed(u % lev, u // lev):
-                        forward(u).wait_send()
-            stiff_out.wait_send()
-            mix_out.wait_send()
-            for k in range(half):
-                state_out(k).wait_send()
+                remote(relay, relay, fs, rr.at[0], (south, lon)).wait_send()
 
     for load in small[:2]:
         load.wait()
@@ -458,6 +481,7 @@
         coef[0, 2 + 2 * r] = jnp.broadcast_to(clon, (8, cols))
 
     adj_load.wait()
+    small[2].wait()
     for level in range(lev):
         tmp[level % 4] = adj[level].astype(jnp.float32)
         for r in range(2):
@@ -483,23 +507,25 @@
 
     @pl.when(even)
     def _():
+        stiff_out.start()
+        when(has_north, lambda: corner_out.start())
         send(0, 0)
         send(0, 2)
 
     @pl.when(odd)
     def _():
+        corner_out.start()
         send(1, 0)
     col_copy(0).start()
 
-    @pl.when(has_north)
-    def _():
-        corner_out.start()
-
-    def give_state(n):
-        tmp[n % 4] = state[nwin - 1, half + n].astype(jnp.float32)
-        for r in range(2):
-            st_out[n, r] = tmp[n % 4, pl.ds(r, spec, stride=2), :]
-        state_out(n).start()
+    def give_state(n, condition=None):
+        def do():
+            tmp[n % 4] = state[nwin - 1, half + n].astype(jnp.float32)
+            for r in range(2):
+                st_out[n, r] = tmp[n % 4, pl.ds(r, spec, stride=2), :]
+            state_out(n).start()
+
+        when(condition, do)
 
     state_loads[nwin - 1].wait()
 
@@ -509,6 +535,7 @@
             if level != 2:
                 send(0, level)
         give_state(0)
+        give_state(1, jnp.logical_not(has_north))
         send(0, half)
         for level in range(half, lev):
             if relayed(level):
@@ -525,7 +552,7 @@
             tall[...] = inv[s].astype(jnp.float32)
             for level in range(lev):
                 mats[s, level] = tall[pl.ds(level, spec, stride=lev), :].T.astype(jnp.bfloat16)
-    for load in small[2:]:
+    for load in small[3:]:
         load.wait()
     for w in range(nwin - 1):
         state_loads[w].wait()
@@ -573,8 +600,7 @@
     @pl.when(even)
     def _():
         mix_out.start()
-        stiff_out.start()
-        give_state(1)
+        give_state(1, has_north)
         for level in range(half + 1, lev):
             if not relayed(level):
                 send(0, level)
@@ -597,24 +623,10 @@
     def _():
         play(1)
 
-    rows_west.wait_send()
-
-    @pl.when(has_north)
-    def _():
-        corner_out.wait_send()
-        for copy in rows_north:
-            copy.wait_send()
-
-    @pl.when(has_south)
-    def _():
-        for copy in rows_out:
-            copy.wait_send()
     with jax.named_scope("reg_end"):
         regions_end()
-    for k in range(1, n_lon):
-        spread(k).wait_send()
-    for k in range(1, n_lat):
-        spread2(k).wait_send()
+    spread_all().wait_send()
+    spread2_all().wait_send()
 
 
 def finish(held_ref, grad_ref, out_hbm, grad_hbm, sems):
@@ -638,6 +650,7 @@
         assert nwin == 2 and rows == 2
         half = lev // 2
         slots = nwin * lev + half
+        passed = sum(relayed(level, w) for level in range(lev) for w in range(nwin))
         lat8 = -(-n_lat // 8) * 8
         f32, bf16 = jnp.float32, jnp.bfloat16
         any_space = pl.BlockSpec(memory_space=pl.ANY)
@@ -667,7 +680,7 @@
                 pltpu.VMEM((spec * lev, spec), f32),
                 pltpu.VMEM(inverses.shape, bf16),
                 blocks(slots), blocks(slots), blocks(slots),
-                blocks(nwin * lev), blocks(nwin * lev), blocks(half), blocks(half), blocks(half),
+                blocks(nwin * lev), blocks(passed), blocks(half), blocks(half), blocks(half),
                 pltpu.VMEM((messages(lev), spec, cols), f32),
                 pltpu.VMEM((messages(lev), spec, cols), f32),
                 pltpu.VMEM(courant_lon.shape, f32),
@@ -689,10 +702,10 @@
                 pltpu.VMEM((n_lat, 1, spec), f32),
                 pltpu.VMEM((n_lat, 1, spec), f32),
                 dma, dma((nwin,)), dma, dma((5,)),
-                dma((slots,)), dma((nwin * lev,)), dma((nwin * lev,)), dma((nwin * lev,)), dma((half,)),
-                dma((half,)), dma((half,)),
-                dma((messages(lev),)), dma((messages(lev),)), dma((8,)), dma((8,)), dma, dma,
-                dma((n_lon,)), dma((n_lon,)), dma((n_lat,)), dma((n_lat,)),
+                dma, dma((nwin * lev,)), dma((passed,)), dma, dma((half,)),
+                dma, dma((half,)),
+                dma, dma((messages(lev),)), dma((8,)), dma((8,)), dma, dma,
+                dma, dma, dma, dma,
             ],
             compiler_params=pltpu.CompilerParams(collective_id=0, has_side_effects=True),
         )(

time: 42.9 us -> 42.2 us (0.984)
  Pallas kernels: 41.9 us -> 41.2 us
    pallas_call x1, Pallas kernels: 41.1 us -> 40.4 us  [per_device(): pl.pallas_call(functools.partial(kernel, n_lat, n_lon), out_shape=(pltpu....]
where the time goes in v2:
time: 42.2 us; the launch traced here: 42 us
  Pallas kernels  41.2 us (98%)
  between operations  0.82 us (2%)
    pallas_call x1, Pallas kernels, per_device(): pl.pallas_call(functools.partial(kernel, n_lat, n_lon), out_shape=(pltpu....  40.4 us

profile of v2, /device:TPU:3, one launch (start us, length us, event | category | flops | bytes accessed | tf_op | source)
XLA Modules:
  0.0 42.0 jit_solution(1745844132892215013)
XLA Ops:
  0.6 40.4 %shard_map.95 = (bf16[8,200,128]{2,1,0:T(8,128)(2,1)S(1)}, f32[1,100]{1,0:T(1,128)S(1)}) custom-call(bf16[8,200,128]{2,1,0:T(8,128)(2,1)} %bitcast.9, bf16[2,8,200,128]{3,2,1,0:T(8,128)(2,1)} %bitcast.7, bf16[3,800,100]{2,1,0:T(8,128)(2,1)} %bitcast.8, f32[2,128]{1,0:T(2,128)} %clon_hbm.1, f32[2,128]{1,0:T(2,128)} %clat_hbm.1, f32[200,128]{1,0:T(8,128)} %bitcast.10, ...), custom_call_target="tpu_custom_call" | custom-call | tf_op jit(solution)/shard_map/pallas_call | solution.py:663
  41.1 0.8 %shard_map.96 = (bf16[8,200,128]{2,1,0:T(8,128)(2,1)}, f32[1,100]{1,0:T(1,128)}) custom-call(bf16[8,200,128]{2,1,0:T(8,128)(2,1)S(1)} %get-tuple-element.6.held_ref, f32[1,100]{1,0:T(1,128)S(1)} %get-tuple-element.7.grad_ref), custom_call_target="tpu_custom_call" | custom-call | tf_op jit(solution)/shard_map/pallas_call | solution.py:717

commit v3 on v2

--- a/solution.py
+++ b/solution.py
@@ -20,26 +20,26 @@
     passed = [l for l in range(half) if relayed(l)]
     passed_merged = [l for l in range(half, lev) if relayed(l)]
     return [
-        ("first", list(range(half, lev))),
+        ("first", list(range(half + 1, lev))),
         ("relay", 0, passed[:1]),
-        ("chem", 1, [(OWN1, l) for l in range(half, lev)]),
+        ("chem", 1, [(OWN1, l) for l in range(half + 1, lev)]),
         ("relay", 0, passed[1:]),
         ("state", 2, half - 1),
-        ("first", list(range(half))),
+        ("first", list(range(half + 1))),
         ("chem", 2, [(OWN1, l) for l in range(half) if not relayed(l)]),
         ("relay", 0, passed_merged),
         ("state", half - 1, half),
         ("move", 1),
-        ("chem", 3, [(OWN1, l) for l in passed]),
+        ("chem", 3, [(OWN1, l) for l in passed + [half]]),
         ("move", 2),
-        ("send", [l for l in range(half, lev) if not relayed(l)]),
+        ("send", [l for l in range(half + 1, lev) if not relayed(l)]),
+        ("relay", 1, passed_merged),
         ("move", 3),
         ("chem", 0, [(OWN0, l) for l in range(half) if not relayed(l)]),
         ("relay", 1, [l for l in range(half) if relayed(l, 1) and not relayed(l)]),
-        ("relay", 1, passed_merged),
+        ("relay", 1, passed),
         ("chem", 0, [(OWN0, l) for l in passed]),
         ("turn",),
-        ("relay", 1, passed),
         ("chem", 0, [(OWN0, l) for l in range(half, lev) if not relayed(l)]),
         ("drain",),
         ("chem", 0, [(OWN0, l) for l in passed_merged]),
@@ -80,7 +80,7 @@
     n_lat, n_lon,
     adj_hbm, state_hbm, inv_hbm, clon_hbm, clat_hbm, em_hbm, reg_hbm, stiff_hbm,
     outbuf, grad_ref,
-    adj, state, inv, clon_ref, clat_ref, em_ref, reg_ref, stiff_ref, tall, mats,
+    adj, state, inv, clon_ref, clat_ref, em_ref, reg_ref, stiff_ref, tall, mats, both,
     lamb, pbuf, vout, vin, relay, zin, st_out, st_in, cout, cin, nclon, nclat, neclat, sclon, sclat, eclat, gstiff, corner_end, corner_in, corner,
     tmp, fin, coef, mixed, part, inbox1, turn, inbox2,
     adj_sem, state_sem, inv_sem, small_sem, vs, vr, rr, fs, zr, ss, sr, cs, cr, ks, kr, ds, dr, s1, r1, s2, r2,
@@ -102,6 +102,8 @@
     has_south = lat < n_lat - 1
     sends_ghost = lat >= 2
     passes_on = lat + 2 < n_lat
+    first_pair = lat < 2
+    later_pair = lat >= 2
     passing = [u for u in range(2 * lev) if relayed(u % lev, u // lev)]
     plans = {0: even_order(lev), 1: odd_order(lev)}
 
@@ -228,7 +230,9 @@
     def own_sends(side, u):
         level = u % lev
         if side == 1:
-            return None if u < lev and level >= half else (direct(u), None)
+            if u == half:
+                return direct(u), later_pair
+            return None if u < lev and level > half else (direct(u), None)
         return (to_relay(u) if relayed(level, u // lev) else direct(u)), has_north
 
     def when(condition, do):
@@ -243,13 +247,21 @@
         with jax.named_scope("move"):
             both = move(u, 1 if kind == GHOST else 0, n, i, combine)
             if combine:
-                if side == 1 and kind == OWN0 and level >= half:
+                merged = side == 1 and kind == OWN0 and level >= half
+                if merged and level > half:
                     ghost = slot_of(GHOST, level)
                     both = both[0] + pbuf[ghost, 0], both[1] + pbuf[ghost, 1]
                 vout[u, 0], vout[u, 1] = both
+                if merged and level == half:
+                    @pl.when(first_pair)
+                    def _():
+                        ghost = slot_of(GHOST, level)
+                        for r in range(2):
+                            vout[u, r] = vout[u, r] + pbuf[ghost, r]
         if kind == GHOST:
-            when(sends_ghost, lambda: ghost_out(level).start())
-        elif kind == OWN0 and not (side == 0 and level >= half and not relayed(level)):
+            if level > half:
+                when(sends_ghost, lambda: ghost_out(level).start())
+        elif kind == OWN0 and not (side == 0 and level > half and not relayed(level)):
             send(side, u)
 
     def send(side, u):
@@ -269,7 +281,7 @@
         if kind == GHOST:
             n = level - half
             with jax.named_scope("w_st"):
-                state_out(n).wait_recv()
+                when(None if n else first_pair, lambda: state_out(n).wait_recv())
             if n == 0:
                 stiff_out.wait_recv()
             x, y, live = [vout[level, r] for r in range(2)], [st_in[n, r] for r in range(2)], gstiff[level]
@@ -279,7 +291,7 @@
                 def _():
                     with jax.named_scope("w_vin"):
                         direct(u).wait_recv()
-                    extra = kind == OWN0 and level >= half
+                    extra = kind == OWN0 and level > half
                     if extra:
                         with jax.named_scope("w_z"):
                             ghost_out(level).wait_recv()
@@ -294,6 +306,14 @@
                 adds = arrived(level) if kind == OWN1 else [vin[u, r] for r in range(2)]
                 x = [pbuf[u, r] + adds[r] for r in range(2)]
             else:
+                if level == half:
+                    @pl.when(later_pair)
+                    def _():
+                        with jax.named_scope("w_vin"):
+                            direct(u).wait_recv()
+                        adds = arrived(level)
+                        for r in range(2):
+                            pbuf[u, r] = pbuf[u, r] + adds[r]
                 x = [pbuf[u, r] for r in range(2)]
             tmp[i] = state[nwin - 1 if kind == OWN1 else 0, level].astype(jnp.float32)
             y, live = [tmp[i, pl.ds(r, spec, stride=2), :] for r in range(2)], stiff_ref[level]
@@ -304,18 +324,27 @@
 
     def chem(levels, gathered):
         flats, ys, lives = zip(*gathered)
+
+        def dot(mat, xs):
+            return [
+                jnp.dot(a, x.astype(jnp.bfloat16), preferred_element_type=jnp.float32) for a, x in zip(mat, xs)]
+
+        v1 = dot([mats[steps - 1, level] for level in levels], flats)
         for s in reversed(range(steps)):
             mat = [mats[s, level] for level in levels]
-
-            def dot(xs):
-                return [jnp.dot(a, x.astype(jnp.bfloat16), preferred_element_type=jnp.float32) for a, x in zip(mat, xs)]
-
-            v1 = dot(flats)
-            v2 = dot([v * y for v, y in zip(v1, ys)])
-            v3 = dot([v * y for v, y in zip(v2, ys)])
+            v2 = dot(mat, [v * y for v, y in zip(v1, ys)])
+            r2 = [v * y for v, y in zip(v2, ys)]
+            v3 = dot(mat, r2)
+            some = [0.4 * x + 0.3 * a + 0.2 * b for x, a, b in zip(flats, v1, v2)]
+            if s:
+                v1 = [
+                    a + b for a, b in zip(
+                        dot([mats[s - 1, level] for level in levels],
+                            [jnp.where(live > s, x, flat) for x, flat, live in zip(some, flats, lives)]),
+                        dot([both[s - 1, level] for level in levels],
+                            [jnp.where(live > s, r, 0.0) for r, live in zip(r2, lives)]))]
             flats = [
-                jnp.where(live > s, 0.4 * x + 0.3 * a + 0.2 * b + 0.1 * c, x)
-                for x, a, b, c, live in zip(flats, v1, v2, v3, lives)
+                jnp.where(live > s, x + 0.1 * c, flat) for x, c, flat, live in zip(some, v3, flats, lives)
             ]
         return flats
 
@@ -382,16 +411,22 @@
         if side == 1:
             left(lev + half)
 
+            @pl.when(later_pair)
+            def _():
+                left(1)
+
             @pl.when(sends_ghost)
             def _():
-                left(half)
+                left(half - 1)
         else:
             @pl.when(has_north)
             def _():
                 left(2 * lev)
             stiff_out.wait_send()
             mix_out.wait_send()
-            remote(st_out, st_in, ss, sr.at[0], (south, lon)).wait_send()
+            n = pl.ds(0, half - 1)
+            remote(st_out.at[n], st_in.at[n], ss, sr.at[0], (south, lon)).wait_send()
+            when(first_pair, lambda: state_out(0).wait_send())
         rows_west.wait_send()
 
         @pl.when(has_north)
@@ -534,8 +569,8 @@
         for level in range(1, half):
             if level != 2:
                 send(0, level)
-        give_state(0)
-        give_state(1, jnp.logical_not(has_north))
+        give_state(0, first_pair)
+        give_state(1, first_pair)
         send(0, half)
         for level in range(half, lev):
             if relayed(level):
@@ -543,7 +578,7 @@
 
     @pl.when(odd)
     def _():
-        for level in range(1, half):
+        for level in range(1, half + 1):
             send(1, level)
 
     inv_load.wait()
@@ -552,6 +587,11 @@
             tall[...] = inv[s].astype(jnp.float32)
             for level in range(lev):
                 mats[s, level] = tall[pl.ds(level, spec, stride=lev), :].T.astype(jnp.bfloat16)
+    with jax.named_scope("both"):
+        for s in range(1, steps):
+            for level in range(lev):
+                both[s - 1, level] = (0.1 * jnp.dot(
+                    mats[s - 1, level], mats[s, level], preferred_element_type=jnp.float32)).astype(jnp.bfloat16)
     for load in small[3:]:
         load.wait()
     for w in range(nwin - 1):
@@ -600,7 +640,7 @@
     @pl.when(even)
     def _():
         mix_out.start()
-        give_state(1, has_north)
+        give_state(1, later_pair)
         for level in range(half + 1, lev):
             if not relayed(level):
                 send(0, level)
@@ -679,6 +719,7 @@
                 pltpu.VMEM(stiffness.shape, jnp.int32),
                 pltpu.VMEM((spec * lev, spec), f32),
                 pltpu.VMEM(inverses.shape, bf16),
+                pltpu.VMEM((steps - 1,) + inverses.shape[1:], bf16),
                 blocks(slots), blocks(slots), blocks(slots),
                 blocks(nwin * lev), blocks(passed), blocks(half), blocks(half), blocks(half),
                 pltpu.VMEM((messages(lev), spec, cols), f32),

time: 42.2 us -> 40.6 us (0.962)
  the two profiles are of different devices: /device:TPU:3 before, /device:TPU:0 now
where the time goes in v3:
time: 40.6 us; the launch traced here: 40.4 us
  Pallas kernels  39.6 us (98%)
  between operations  0.82 us (2%)
    pallas_call x1, Pallas kernels, per_device(): pl.pallas_call(functools.partial(kernel, n_lat, n_lon), out_shape=(pltpu....  38.8 us

profile of v3, /device:TPU:0, one launch (start us, length us, event | category | flops | bytes accessed | tf_op | source)
XLA Modules:
  0.0 40.4 jit_solution(9970629004723122938)
XLA Ops:
  0.6 38.8 %shard_map.95 = (bf16[8,200,128]{2,1,0:T(8,128)(2,1)S(1)}, f32[1,100]{1,0:T(1,128)S(1)}) custom-call(bf16[8,200,128]{2,1,0:T(8,128)(2,1)} %bitcast.9, bf16[2,8,200,128]{3,2,1,0:T(8,128)(2,1)} %bitcast.7, bf16[3,800,100]{2,1,0:T(8,128)(2,1)} %bitcast.8, f32[2,128]{1,0:T(2,128)} %clon_hbm.1, f32[2,128]{1,0:T(2,128)} %clat_hbm.1, f32[200,128]{1,0:T(8,128)} %bitcast.10, ...), custom_call_target="tpu_custom_call" | custom-call | tf_op jit(solution)/shard_map/pallas_call | solution.py:703
  39.4 0.8 %shard_map.96 = (bf16[8,200,128]{2,1,0:T(8,128)(2,1)}, f32[1,100]{1,0:T(1,128)}) custom-call(bf16[8,200,128]{2,1,0:T(8,128)(2,1)S(1)} %get-tuple-element.6.held_ref, f32[1,100]{1,0:T(1,128)S(1)} %get-tuple-element.7.grad_ref), custom_call_target="tpu_custom_call" | custom-call | tf_op jit(solution)/shard_map/pallas_call | solution.py:758

commit v4 on v3

--- a/solution.py
+++ b/solution.py
@@ -41,8 +41,10 @@
         ("chem", 0, [(OWN0, l) for l in passed]),
         ("turn",),
         ("chem", 0, [(OWN0, l) for l in range(half, lev) if not relayed(l)]),
+        ("chem", 0, [(OWN0, l) for l in passed_merged[:-1]]),
         ("drain",),
-        ("chem", 0, [(OWN0, l) for l in passed_merged]),
+        ("chem", 0, [(OWN0, l) for l in passed_merged[-1:]]),
+        ("end",),
     ]
 
 
@@ -68,8 +70,17 @@
         ("turn",),
         ("chem", 0, [(OWN0, m + 1), (OWN0, m + 2)]),
         ("drain",),
+        ("end",),
         ("chem", 0, [(OWN0, 2), (OWN0, 3), (OWN0, m + 3)]),
     ]
+
+
+def corners(lev):
+    return {
+        level: (op[1], i)
+        for op in odd_order(lev) if op[0] == "chem"
+        for i, (kind, level) in enumerate(op[2]) if kind == OWN1 and level < lev // 2
+    }
 
 
 def messages(lev):
@@ -81,9 +92,9 @@
     adj_hbm, state_hbm, inv_hbm, clon_hbm, clat_hbm, em_hbm, reg_hbm, stiff_hbm,
     outbuf, grad_ref,
     adj, state, inv, clon_ref, clat_ref, em_ref, reg_ref, stiff_ref, tall, mats, both,
-    lamb, pbuf, vout, vin, relay, zin, st_out, st_in, cout, cin, nclon, nclat, neclat, sclon, sclat, eclat, gstiff, corner_end, corner_in, corner,
+    lamb, pbuf, vout, vin, relay, zin, st_out, st_in, cout, cin, nclon, nclat, neclat, sclon, sclat, eclat, gstiff, corner_all, late_end, late_in, corner_end, corner_in, corner,
     tmp, fin, coef, mixed, part, inbox1, turn, inbox2,
-    adj_sem, state_sem, inv_sem, small_sem, vs, vr, rr, fs, zr, ss, sr, cs, cr, ks, kr, ds, dr, s1, r1, s2, r2,
+    adj_sem, state_sem, inv_sem, small_sem, vs, vr, rr, fs, zr, ss, sr, cs, cr, ks, kr, ds, dr, ds2, dr2, s1, r1, s2, r2,
 ):
     lev, rows2, cols = adj.shape
     nwin = state.shape[0]
@@ -156,11 +167,11 @@
         return pltpu.make_async_remote_copy(
             src_ref=src, dst_ref=dst, send_sem=send, recv_sem=recv, device_id=to, device_id_type=MESH)
 
-    def leaves(u):
-        return (lamb if u < lev else vout).at[u]
-
-    def direct(u):
-        return remote(leaves(u), vin.at[u], vs, vr.at[u], (north, lon))
+    def leaves(u, raw=False):
+        return (lamb if u < lev or raw else vout).at[u]
+
+    def direct(u, raw=False):
+        return remote(leaves(u, raw), vin.at[u], vs, vr.at[u], (north, lon))
 
     def to_relay(u):
         n = passing.index(u)
@@ -232,7 +243,7 @@
         if side == 1:
             if u == half:
                 return direct(u), later_pair
-            return None if u < lev and level > half else (direct(u), None)
+            return None if u < lev and level > half else (direct(u, level < half), None)
         return (to_relay(u) if relayed(level, u // lev) else direct(u)), has_north
 
     def when(condition, do):
@@ -243,7 +254,8 @@
 
     def transport(side, n, i, kind, level):
         u = slot_of(kind, level)
-        combine = kind != OWN1 or (side == 1 and level >= half)
+        raw = side == 1 and kind == OWN0 and level < half
+        combine = (kind != OWN1 or (side == 1 and level >= half)) and not raw
         with jax.named_scope("move"):
             both = move(u, 1 if kind == GHOST else 0, n, i, combine)
             if combine:
@@ -261,7 +273,7 @@
         if kind == GHOST:
             if level > half:
                 when(sends_ghost, lambda: ghost_out(level).start())
-        elif kind == OWN0 and not (side == 0 and level > half and not relayed(level)):
+        elif kind == OWN0 and not raw and not (side == 0 and level > half and not relayed(level)):
             send(side, u)
 
     def send(side, u):
@@ -269,10 +281,20 @@
         if leaving is not None:
             when(leaving[1], lambda: leaving[0].start())
 
-    def arrived(level):
+    def corner_late(n):
+        return remote(late_end.at[n], late_in.at[n], ds2, dr2.at[n], (north, west))
+
+    def arrived(level, u=None):
         al, be, ga, de = [mixed[k, 0:1, :] for k in range(4)]
-        row0, row1, message = vin[level, 0], vin[level, 1], corner[...]
-        edge = message if level == 0 else pltpu.roll(message, cols - 4 * level, 1)
+        if u is None:
+            u, message, at = level, corner[...], level
+        else:
+            n, i = corners(lev)[level]
+            corner_late(n - 1).wait_recv()
+            message, at = jnp.concatenate(
+                [late_in[n - 1], jnp.zeros((cols - 8, cols), jnp.float32)], axis=0).T[:spec], 4 * i
+        row0, row1 = vin[u, 0], vin[u, 1]
+        edge = message if at == 0 else pltpu.roll(message, cols - at, 1)
         right0 = after(jnp.where(lane == 0, edge, row0))
         return al * row0, be * row0 + ga * row1 + de * right0
 
@@ -303,7 +325,12 @@
             elif kind == OWN0 or level < half:
                 with jax.named_scope("w_vin"):
                     direct(u).wait_recv()
-                adds = arrived(level) if kind == OWN1 else [vin[u, r] for r in range(2)]
+                if kind == OWN1:
+                    adds = arrived(level)
+                elif level < half:
+                    adds = arrived(level, u)
+                else:
+                    adds = [vin[u, r] for r in range(2)]
                 x = [pbuf[u, r] + adds[r] for r in range(2)]
             else:
                 if level == half:
@@ -410,6 +437,7 @@
 
         if side == 1:
             left(lev + half)
+            remote(late_end, late_in, ds2, dr2.at[0], (north, west)).wait_send()
 
             @pl.when(later_pair)
             def _():
@@ -455,9 +483,15 @@
                         for r in range(2):
                             lamb[u, r] = flat[:, r * cols:(r + 1) * cols]
                         slots.append((u, 1 if kind == GHOST else 0))
+                        if side == 1 and kind == OWN1 and level < half:
+                            send(side, u)
                     with jax.named_scope("pack"):
                         pack(n, slots)
                     col_copy(n).start()
+                    if side == 1 and n in [m for m, _ in corners(lev).values()]:
+                        late_end[n - 1] = jnp.concatenate(
+                            [cout[n], jnp.zeros((cols - spec, cols), jnp.float32)], axis=0).T[:8]
+                        corner_late(n - 1).start()
                     sent[n] = [(OWN0 if kind == OWN1 else GHOST, level) for kind, level in items]
                 else:
                     for i, ((kind, level), flat) in enumerate(zip(items, flats)):
@@ -497,6 +531,11 @@
                     give_state(k)
             elif op[0] == "drain":
                 drain(side, sent)
+            elif op[0] == "end":
+                with jax.named_scope("reg_end"):
+                    regions_end()
+                spread_all().wait_send()
+                spread2_all().wait_send()
             else:
                 with jax.named_scope("turn"):
                     regions_turn()
@@ -523,8 +562,9 @@
             lamb[level, r] = tmp[level % 4, pl.ds(r, spec, stride=2), :]
     with jax.named_scope("pack"):
         pack(0, [(level, 0) for level in range(lev)])
-        corner_end[...] = jnp.concatenate(
+        corner_all[...] = jnp.concatenate(
             [cout[0], jnp.zeros((cols - spec, cols), jnp.float32)], axis=0).T[:4 * lev]
+        corner_end[...] = corner_all[pl.ds(0, lev, stride=4), :]
     with jax.named_scope("w_barrier"):
         pl.semaphore_wait(
             barrier, n_lon - 1 + n_lat - 1 + 2 * has_north.astype(jnp.int32) + 2 * has_south.astype(jnp.int32))
@@ -650,7 +690,7 @@
         with jax.named_scope("w_corner"):
             corner_out.wait_recv()
         corner[...] = jnp.concatenate(
-            [corner_in[...], jnp.zeros((cols - 4 * lev, cols), jnp.float32)], axis=0).T[:spec]
+            [corner_in[...], jnp.zeros((cols - lev, cols), jnp.float32)], axis=0).T[:spec]
 
     with jax.named_scope("w_col"):
         col_copy(0).wait_recv()
@@ -662,11 +702,6 @@
     @pl.when(odd)
     def _():
         play(1)
-
-    with jax.named_scope("reg_end"):
-        regions_end()
-    spread_all().wait_send()
-    spread2_all().wait_send()
 
 
 def finish(held_ref, grad_ref, out_hbm, grad_hbm, sems):
@@ -732,7 +767,10 @@
                 pltpu.VMEM(courant_lat.shape, f32),
                 pltpu.VMEM(stiffness.shape, jnp.int32),
                 pltpu.VMEM((4 * lev, cols), f32),
-                pltpu.VMEM((4 * lev, cols), f32),
+                pltpu.VMEM((half, 8, cols), f32),
+                pltpu.VMEM((half, 8, cols), f32),
+                pltpu.VMEM((lev, cols), f32),
+                pltpu.VMEM((lev, cols), f32),
                 pltpu.VMEM((spec, cols), f32),
                 pltpu.VMEM((4, rows * spec, cols), f32),
                 pltpu.VMEM((spec, rows * cols), f32),
@@ -745,7 +783,7 @@
                 dma, dma((nwin,)), dma, dma((5,)),
                 dma, dma((nwin * lev,)), dma((passed,)), dma, dma((half,)),
                 dma, dma((half,)),
-                dma, dma((messages(lev),)), dma((8,)), dma((8,)), dma, dma,
+                dma, dma((messages(lev),)), dma((8,)), dma((8,)), dma, dma, dma, dma((half,)),
                 dma, dma, dma, dma,
             ],
             compiler_params=pltpu.CompilerParams(collective_id=0, has_side_effects=True),

time: 40.6 us -> 40.1 us (0.988)
  Pallas kernels: 39.6 us -> 39.1 us
    pallas_call x1, Pallas kernels: 38.8 us -> 38.3 us  [per_device(): pl.pallas_call(functools.partial(kernel, n_lat, n_lon), out_shape=(pltpu....]
where the time goes in v4:
time: 40.1 us; the launch traced here: 39.9 us
  Pallas kernels  39.1 us (98%)
  between operations  0.82 us (2%)
    pallas_call x1, Pallas kernels, per_device(): pl.pallas_call(functools.partial(kernel, n_lat, n_lon), out_shape=(pltpu....  38.3 us

profile of v4, /device:TPU:0, one launch (start us, length us, event | category | flops | bytes accessed | tf_op | source)
XLA Modules:
  0.0 39.9 jit_solution(5353430477288439452)
XLA Ops:
  0.6 38.3 %shard_map.95 = (bf16[8,200,128]{2,1,0:T(8,128)(2,1)S(1)}, f32[1,100]{1,0:T(1,128)S(1)}) custom-call(bf16[8,200,128]{2,1,0:T(8,128)(2,1)} %bitcast.9, bf16[2,8,200,128]{3,2,1,0:T(8,128)(2,1)} %bitcast.7, bf16[3,800,100]{2,1,0:T(8,128)(2,1)} %bitcast.8, f32[2,128]{1,0:T(2,128)} %clon_hbm.1, f32[2,128]{1,0:T(2,128)} %clat_hbm.1, f32[200,128]{1,0:T(8,128)} %bitcast.10, ...), custom_call_target="tpu_custom_call" | custom-call | tf_op jit(solution)/shard_map/pallas_call | solution.py:738
  38.9 0.8 %shard_map.96 = (bf16[8,200,128]{2,1,0:T(8,128)(2,1)}, f32[1,100]{1,0:T(1,128)}) custom-call(bf16[8,200,128]{2,1,0:T(8,128)(2,1)S(1)} %get-tuple-element.6.held_ref, f32[1,100]{1,0:T(1,128)S(1)} %get-tuple-element.7.grad_ref), custom_call_target="tpu_custom_call" | custom-call | tf_op jit(solution)/shard_map/pallas_call | solution.py:796

commit v5 on v4

--- a/solution.py
+++ b/solution.py
@@ -94,7 +94,7 @@
     adj, state, inv, clon_ref, clat_ref, em_ref, reg_ref, stiff_ref, tall, mats, both,
     lamb, pbuf, vout, vin, relay, zin, st_out, st_in, cout, cin, nclon, nclat, neclat, sclon, sclat, eclat, gstiff, corner_all, late_end, late_in, corner_end, corner_in, corner,
     tmp, fin, coef, mixed, part, inbox1, turn, inbox2,
-    adj_sem, state_sem, inv_sem, small_sem, vs, vr, rr, fs, zr, ss, sr, cs, cr, ks, kr, ds, dr, ds2, dr2, s1, r1, s2, r2,
+    adj_sem, state_sem, inv_sem, small_sem, vs, vr, rr, fs, ss, cs, cr, ks, kr, ds, dr, ds2, dr2, s1, r1, s2, r2,
 ):
     lev, rows2, cols = adj.shape
     nwin = state.shape[0]
@@ -182,27 +182,31 @@
 
     def ghost_out(level):
         u, n = slot_of(GHOST, level), level - half
-        return remote(vout.at[u], zin.at[n], vs, zr.at[n], (north2, lon))
+        return remote(vout.at[u], zin.at[n], vs, rr.at[half + n], (north2, lon))
 
     def state_out(n):
-        return remote(st_out.at[n], st_in.at[n], ss, sr.at[n], (south, lon))
+        return remote(st_out.at[n], st_in.at[n], ss, rr.at[n], (south, lon))
 
     def col_copy(n):
         return remote(cout.at[n], cin.at[n], cs, cr.at[n], (lat, west))
 
     rows_out = [
         remote(clon_ref, nclon, ks.at[0], kr.at[0], (south, lon)),
-        remote(clat_ref, nclat, ks.at[1], kr.at[1], (south, lon)),
-        remote(clat_ref, neclat, ks.at[2], kr.at[2], (south, west)),
+        remote(clat_ref, nclat, ks.at[0], kr.at[0], (south, lon)),
+        remote(clat_ref, neclat, ks.at[0], kr.at[0], (south, west)),
     ]
     rows_north = [
-        remote(clon_ref, sclon, ks.at[5], kr.at[5], (north, lon)),
-        remote(clat_ref, sclat, ks.at[6], kr.at[6], (north, lon)),
+        remote(clon_ref, sclon, ks.at[0], kr.at[1], (north, lon)),
+        remote(clat_ref, sclat, ks.at[0], kr.at[1], (north, lon)),
     ]
-    rows_west = remote(clat_ref, eclat, ks.at[7], kr.at[7], (lat, west))
+    rows_west = remote(clat_ref, eclat, ks.at[0], kr.at[2], (lat, west))
     corner_out = remote(corner_end, corner_in, ds, dr, (north, west))
-    stiff_out = remote(stiff_ref, gstiff, ks.at[3], kr.at[3], (south, lon))
-    mix_out = remote(coef.at[0, pl.ds(5, 4)], coef.at[1, pl.ds(5, 4)], ks.at[4], kr.at[4], (south, lon))
+
+    def row_copies(n, recv):
+        return remote(stiff_ref.at[pl.ds(0, n)], gstiff.at[pl.ds(0, n)], ks.at[0], kr.at[recv], (south, lon))
+
+    stiff_out = remote(stiff_ref, gstiff, ks.at[1], kr.at[3], (south, lon))
+    mix_out = remote(coef.at[0, pl.ds(5, 4)], coef.at[1, pl.ds(5, 4)], ks.at[2], kr.at[4], (south, lon))
 
     def after(x):
         return pltpu.roll(x, cols - 1, 1)
@@ -453,20 +457,18 @@
             stiff_out.wait_send()
             mix_out.wait_send()
             n = pl.ds(0, half - 1)
-            remote(st_out.at[n], st_in.at[n], ss, sr.at[0], (south, lon)).wait_send()
+            remote(st_out.at[n], st_in.at[n], ss, rr.at[0], (south, lon)).wait_send()
             when(first_pair, lambda: state_out(0).wait_send())
         rows_west.wait_send()
 
         @pl.when(has_north)
         def _():
             corner_out.wait_send()
-            for copy in rows_north:
-                copy.wait_send()
+            row_copies(len(rows_north), 1).wait_send()
 
         @pl.when(has_south)
         def _():
-            for copy in rows_out:
-                copy.wait_send()
+            row_copies(len(rows_out), 0).wait_send()
 
     def play(side):
         sent = {}
@@ -644,8 +646,7 @@
 
     @pl.when(has_north)
     def _():
-        for copy in rows_out:
-            copy.wait_recv()
+        row_copies(len(rows_out), 0).wait_recv()
         c0, o0, n0 = coef[0, 0], coef[0, 2], coef[0, 1]
         for r in range(2):
             clon, clat = nclon[r:r + 1, :], nclat[r:r + 1, :]
@@ -668,8 +669,7 @@
 
     @pl.when(has_south)
     def _():
-        for copy in rows_north:
-            copy.wait_recv()
+        row_copies(len(rows_north), 1).wait_recv()
         clon, clat = sclon[0:1, :], sclat[0:1, :]
         below = jnp.broadcast_to(clat_ref[1:2, :], (8, cols))
         mixed[0] = coef[0, 1] * below
@@ -781,9 +781,9 @@
                 pltpu.VMEM((n_lat, 1, spec), f32),
                 pltpu.VMEM((n_lat, 1, spec), f32),
                 dma, dma((nwin,)), dma, dma((5,)),
-                dma, dma((nwin * lev,)), dma((passed,)), dma, dma((half,)),
-                dma, dma((half,)),
-                dma, dma((messages(lev),)), dma((8,)), dma((8,)), dma, dma, dma, dma((half,)),
+                dma, dma((nwin * lev,)), dma((max(passed, 2 * half),)), dma,
+                dma,
+                dma, dma((messages(lev),)), dma((3,)), dma((5,)), dma, dma, dma, dma((half,)),
                 dma, dma, dma, dma,
             ],
             compiler_params=pltpu.CompilerParams(collective_id=0, has_side_effects=True),

time: 40.1 us -> 39.9 us (level)
  no operation moved by 1% of the time
where the time goes in v5:
time: 39.9 us; the launch traced here: 39.8 us
  Pallas kernels  38.9 us (97%)
  between operations  0.82 us (2%)
    pallas_call x1, Pallas kernels, per_device(): pl.pallas_call(functools.partial(kernel, n_lat, n_lon), out_shape=(pltpu....  38.2 us

profile of v5, /device:TPU:0, one launch (start us, length us, event | category | flops | bytes accessed | tf_op | source)
XLA Modules:
  0.0 39.8 jit_solution(17580534441592926179)
XLA Ops:
  0.6 38.2 %shard_map.95 = (bf16[8,200,128]{2,1,0:T(8,128)(2,1)S(1)}, f32[1,100]{1,0:T(1,128)S(1)}) custom-call(bf16[8,200,128]{2,1,0:T(8,128)(2,1)} %bitcast.9, bf16[2,8,200,128]{3,2,1,0:T(8,128)(2,1)} %bitcast.7, bf16[3,800,100]{2,1,0:T(8,128)(2,1)} %bitcast.8, f32[2,128]{1,0:T(2,128)} %clon_hbm.1, f32[2,128]{1,0:T(2,128)} %clat_hbm.1, f32[200,128]{1,0:T(8,128)} %bitcast.10, ...), custom_call_target="tpu_custom_call" | custom-call | tf_op jit(solution)/shard_map/pallas_call | solution.py:738
  38.8 0.8 %shard_map.96 = (bf16[8,200,128]{2,1,0:T(8,128)(2,1)}, f32[1,100]{1,0:T(1,128)}) custom-call(bf16[8,200,128]{2,1,0:T(8,128)(2,1)S(1)} %get-tuple-element.6.held_ref, f32[1,100]{1,0:T(1,128)S(1)} %get-tuple-element.7.grad_ref), custom_call_target="tpu_custom_call" | custom-call | tf_op jit(solution)/shard_map/pallas_call | solution.py:796
